TPU v7x, 512 devices: a whole 4x4x16 slice. The times are simulated.
512 devices in a mesh: sym: 8 (over y, core), tile: 64 (over z, x).
Axes of the slice: x: 4, y: 4, z: 16, core: 2. Of those that a mesh axis runs over, the one named last changes fastest.
Arguments:
- amplitudes: bfloat16 [256, 131072], P(None, ('sym', 'tile')), may hold values from -6 to 6
- slot_cols: int32 [1024, 64], P(('sym', 'tile')), may hold values from 0 to 127, as said below
- slot_count: int32 [1024], P(('sym', 'tile')), may hold values from 16 to 64, as said below
- integrals: bfloat16 [1024, 64, 128, 128], P(('sym', 'tile')), may hold values from -0.0625 to 0.0625
- cycle_same: bfloat16 [8, 128, 128], P('sym'), may hold values from -0.375 to 0.375
- cycle_cross: bfloat16 [8, 128, 128], P('sym'), may hold values from -0.375 to 0.375
Outputs:
- residual: bfloat16 [256, 131072], P(None, ('sym', 'tile'))
Inputs may be any that keep to these rules, and one draw needn't show every extreme that they name: `slot_cols`: tile index within the symmetry block; the live entries of a row are distinct and rising. `slot_count`: some virtual-pair tile has all 64 slots live.
All inputs are finite; a program needn't handle non-finite values.
Results may differ from a plain program's by a relative error of at most 0.0044.
Values may be sent and summed in bfloat16 or wider, within the bound.
A program may use at most 128 MiB of HBM per device.

v0:
```python
import jax
import jax.numpy as jnp
from jax import lax
from jax.sharding import PartitionSpec as P


def from_partner(value, axis, bit):
    mask = 2**bit
    pairs = [(source, source ^ mask) for source in range(lax.axis_size(axis))]
    return lax.ppermute(value, axis, pairs)


def cycle_rows(same_rows, cross_rows, own_part, other_part, block_tiles, tile_width):
    items = own_part.shape[0]
    own_three = own_part.reshape(items, block_tiles, tile_width)
    other_three = other_part.reshape(items, block_tiles, tile_width)
    result = jnp.einsum("uv,pva->pua", same_rows, own_three, preferred_element_type=jnp.float32)
    result = result + jnp.einsum(
        "uv,pva->pua", cross_rows, other_three, preferred_element_type=jnp.float32
    )
    return result


def on_device(amplitudes, slot_cols, slot_count, integrals, cycle_same, cycle_cross):
    pair_count = amplitudes.shape[0]
    rows_local = integrals.shape[0]
    slot_total = integrals.shape[1]
    tile_width = integrals.shape[3]
    block_tiles = cycle_same.shape[1]
    gathered = lax.all_gather(amplitudes, "tile", axis=1, tiled=True)
    block_three = gathered.reshape(pair_count, block_tiles, tile_width)
    live_slot = lax.broadcasted_iota(jnp.int32, (rows_local, slot_total), 1) < slot_count[:, None]
    take_index = jnp.where(live_slot, slot_cols, block_tiles)
    ladder_parts = []
    for tile_row in range(rows_local):
        picked = jnp.take(block_three, take_index[tile_row], axis=1, mode="fill", fill_value=0)
        ladder_parts.append(
            jnp.einsum(
                "psc,sac->pa", picked, integrals[tile_row], preferred_element_type=jnp.float32
            )
        )
    ladder = jnp.stack(ladder_parts, axis=1).reshape(pair_count, rows_local * tile_width)
    dressed = (amplitudes.astype(jnp.float32) + ladder).astype(jnp.bfloat16)
    partner = from_partner(dressed, "sym", 0)
    whole_own, whole_partner = (
        lax.all_gather(dressed, "tile", axis=1, tiled=True),
        lax.all_gather(partner, "tile", axis=1, tiled=True),
    )
    position = lax.axis_index("tile")
    same_rows = lax.dynamic_slice_in_dim(cycle_same[0], position * rows_local, rows_local, 0)
    cross_rows = lax.dynamic_slice_in_dim(cycle_cross[0], position * rows_local, rows_local, 0)
    cycle_term = cycle_rows(
        same_rows, cross_rows, whole_own, whole_partner, block_tiles, tile_width
    )
    cycle_term = cycle_term.reshape(pair_count, rows_local * tile_width)
    return (ladder + cycle_term).astype(jnp.bfloat16)


def solution(mesh):
    in_specs = (
        P(None, ("sym", "tile")),
        P(("sym", "tile"), None),
        P(("sym", "tile")),
        P(("sym", "tile"), None, None, None),
        P("sym", None, None),
        P("sym", None, None),
    )
    out_specs = P(None, ("sym", "tile"))
    return jax.shard_map(
        on_device, mesh=mesh, in_specs=in_specs, out_specs=out_specs, check_vma=False
    )
```

profile of v0, /device:TPU:24, one launch (start us, length us, event | category | flops | bytes accessed | tf_op | source)
XLA Modules:
  0.0 553.6 jit_solution(9314749196532757080)
XLA Ops:
  6.5 0.0 copy-start
  6.5 0.0 all-gather.4.cloned.1.call-start
  6.5 1.7 copy.11
  8.2 0.0 all-gather.4.cloned.1.call-update
  8.2 0.0 all-gather.6.cloned.1.call-start
  8.3 0.8 compare_select_fusion.2
  9.1 161.4 %all-gather.4.cloned.1.call-done = bf16[256,16384]{0,1:T(8,128)(2,1)} async-done(((bf16[256,256]{0,1:T(8,128)(2,1)}), bf16[256,16384]{0,1:T(8,128)(2,1)}) %all-gather.4.cloned.1.call-update) | async-done | bytes 8388624 | tf_op jit(solution)/shard_map/all_gather | solution.py:30
  170.5 12.0 %copy.12 = bf16[256,128,128]{2,0,1:T(8,128)(2,1)} copy(bf16[256,128,128]{0,2,1:T(8,128)(2,1)} %bitcast.58) | data formatting | bytes 16777216 | tf_op jit(solution)/shard_map/reshape | solution.py:31
  182.4 6.4 %gather_fusion.1 = bf16[64,256,128]{2,1,0:T(8,128)(2,1)} fusion(bf16[256,128,128]{2,0,1:T(8,128)(2,1)} %copy.12, s32[1024]{0:T(1024)S(1)} %get-tuple-element.12), kind=kCustom, calls=%fused_computation.1.clone | custom fusion | bytes 8388864 | tf_op jit(solution)/shard_map/jit(_take)/gather | solution.py:36
  188.9 6.4 %gather_fusion = bf16[64,256,128]{2,1,0:T(8,128)(2,1)} fusion(bf16[256,128,128]{2,0,1:T(8,128)(2,1)} %copy.12, s32[1024]{0:T(1024)S(1)} %get-tuple-element.13), kind=kCustom, calls=%fused_computation.clone | custom fusion | bytes 8388864 | tf_op jit(solution)/shard_map/jit(_take)/gather | solution.py:36
  195.3 0.0 copy-start.1
  195.3 4.6 fusion.14
  199.8 0.0 copy-done.1
  199.8 0.8 copy-done.4
  200.6 1.6 fusion.19
  202.2 0.1 copy.15
  202.3 0.0 copy-done.2
  202.3 0.7 add_convert_fusion
  203.0 0.0 all-gather.6.cloned.1.call-update
  203.1 0.0 all-gather.8.cloned.1.call-start
  203.1 1.9 collective-permute-start
  205.0 1.5 collective-permute-done
  206.6 0.6 copy-done.3
  207.2 0.0 all-gather.8.cloned.1.call-update
  207.2 159.4 %all-gather.6.cloned.1.call-done = bf16[256,16384]{1,0:T(8,128)(2,1)} async-done(((bf16[256,256]{1,0:T(8,128)(2,1)}), bf16[256,16384]{1,0:T(8,128)(2,1)}) %all-gather.6.cloned.1.call-update) | async-done | bytes 8388624 | tf_op jit(solution)/shard_map/all_gather | solution.py:46
  366.6 9.2 %copy.16 = bf16[32,8,128,128]{3,2,1,0:T(8,128)(2,1)} copy(bf16[32,8,128,128]{3,1,2,0:T(8,128)(2,1)} %bitcast.56) | data formatting | bytes 16777216
  375.8 0.0 copy-done
  375.8 4.6 fusion.26
  380.4 152.2 %all-gather.8.cloned.1.call-done = bf16[256,16384]{1,0:T(8,128)(2,1)} async-done(((bf16[256,256]{1,0:T(8,128)(2,1)}), bf16[256,16384]{1,0:T(8,128)(2,1)}) %all-gather.8.cloned.1.call-update) | async-done | bytes 8388624 | tf_op jit(solution)/shard_map/all_gather | solution.py:47
  532.6 9.2 %copy.17 = bf16[32,8,128,128]{3,2,1,0:T(8,128)(2,1)} copy(bf16[32,8,128,128]{3,1,2,0:T(8,128)(2,1)} %bitcast.57) | data formatting | bytes 16777216
  541.8 4.6 convolution_add_fusion
  546.4 0.7 fusion.24
  (6 shorter events, 0.0 us)
Async XLA Ops:
  6.5 369.3 %copy-start = (bf16[1,128,128]{2,1,0:T(8,128)(2,1)S(1)}, bf16[1,128,128]{2,1,0:T(8,128)(2,1)}, u32[]{:S(2)}) copy-start(bf16[1,128,128]{2,1,0:T(8,128)(2,1)} %param.12) | copy-start | bytes 98308
  6.5 163.9 %all-gather.4.cloned.1.call-start = ((), (), s32[]{:S(2)}) async-start(), calls=%async_computation | async-start | bytes 8519680 | tf_op jit(solution)/shard_map/all_gather | solution.py:30
  8.2 358.4 %all-gather.6.cloned.1.call-start = ((), (), s32[]{:S(2)}) async-start(), calls=%async_computation.1 | async-start | bytes 8519680 | tf_op jit(solution)/shard_map/all_gather | solution.py:46
  195.3 4.6 copy-start.1
  195.3 5.3 copy-start.4
  200.6 1.7 copy-start.2
  203.1 329.6 %all-gather.8.cloned.1.call-start = ((), (), s32[]{:S(2)}) async-start(), calls=%async_computation.2 | async-start | bytes 8519680 | tf_op jit(solution)/shard_map/all_gather | solution.py:47
  203.1 3.5 collective-permute-start
  206.6 0.6 copy-start.3
Sparse Core Ops, SparseCore 0:
  10.3 160.1 all-gather.3
  203.2 163.4 all-gather.5
  369.6 163.0 all-gather.7
where the time goes:
time: 554 us
  waiting for transfers between devices  475 us (86%)
  local copies, waits for them, and re-layouts  46.4 us (8%)
  matrix products  15.3 us (3%)
  between operations  13.2 us (2%)
    all_gather x1, waiting for transfers between devices, on_device(): gathered = lax.all_gather(amplitudes, 'tile', axis=1, tiled=True)  161 us
    all_gather x1, waiting for transfers between devices, on_device(): lax.all_gather(dressed, 'tile', axis=1, tiled=True)  159 us
    all_gather x1, waiting for transfers between devices, on_device(): lax.all_gather(partner, 'tile', axis=1, tiled=True)  152 us
    unnamed x13, local copies, waits for them, and re-layouts  21.5 us
    gather x2, local copies, waits for them, and re-layouts, on_device(): jnp.take(block_three, take_index[tile_row], axis=1, mode='fill', fill_val...  12.8 us
    reshape x1, local copies, waits for them, and re-layouts, on_device(): block_three = gathered.reshape(pair_count, block_tiles, tile_width)  12 us
  transfers between devices with their start and end apart: 4, of which 4 were waited for; matrix products, arithmetic and copies ran while one was open for 3% of the time, Pallas kernels for 0%

commit v1 on v0

v1 whole, which is shorter than its diff:
```python
import functools

import jax
import jax.numpy as jnp
from jax import lax
from jax.experimental import pallas as pl
from jax.experimental.pallas import tpu as pltpu
from jax.sharding import PartitionSpec as P

MESH = pl.DeviceIdType.MESH
NX = 4
F32 = jnp.float32
BF16 = jnp.bfloat16


def nt_dot(a, b):
    return lax.dot_general(a, b, (((1,), (1,)), ((), ())), preferred_element_type=F32)


def kernel(
    nz, ra, idx, amps, integ, same, cross, out,
    ga, gb, iv, cv, lm, km, av, acc, acc2, ds, e, rs, r,
    loc, zb_s, zb_r, za_s, za_r, xa_s, xa_r, xb_s, xb_r,
    zd_s, zd_r, xe_s, xe_r, pe_s, pe_r, zr_s, zr_r,
):
    nh = nz // 2
    pairs, width = amps.shape
    rb = pairs - ra
    tw = width // 2
    ps = pairs // nz
    slots = integ.shape[1]
    t = lax.axis_index("tile")
    g = lax.axis_index("sym")
    z, x = t // NX, t % NX
    xl, xr, xo = (x + NX - 1) % NX, (x + 1) % NX, (x + 2) % NX
    xn = (xr, xl)
    zn = ((z + 1) % nz, (z + nz - 1) % nz)
    dev_z = [{"tile": zz * NX + x} for zz in zn]
    dev_x = [{"tile": z * NX + xx} for xx in xn]
    dev_p = {"sym": g + 1 - 2 * (g % 2)}

    def rc(src, dst, ss, rr, dev):
        return pltpu.make_async_remote_copy(
            src_ref=src, dst_ref=dst, send_sem=ss, recv_sem=rr, device_id=dev, device_id_type=MESH
        )

    bar = pltpu.get_barrier_semaphore()
    for dev in dev_z + dev_x + [dev_p]:
        pl.semaphore_signal(bar, inc=1, device_id=dev, device_id_type=MESH)
    pl.semaphore_wait(bar, 5)

    own_a = amps.at[pl.ds(0, ra), :]
    own_b = amps.at[pl.ds(ra, rb), :]
    for d in range(2):
        rc(own_b, gb.at[z, x], zb_s.at[d, 1], zb_r.at[d, 1], dev_z[d]).start()
        rc(own_a, ga.at[z, x], xa_s.at[d], xa_r.at[d], dev_x[d]).start()
    for d in range(2):
        rc(own_b, gb.at[z, x], xb_s.at[0, d], xb_r.at[0, d], dev_x[d]).start()
    local = [
        pltpu.make_async_copy(own_a, ga.at[z, x], loc.at[0]),
        pltpu.make_async_copy(own_b, gb.at[z, x], loc.at[1]),
        pltpu.make_async_copy(amps, av, loc.at[2]),
        pltpu.make_async_copy(same.at[0], cv.at[0], loc.at[3]),
        pltpu.make_async_copy(cross.at[0], cv.at[1], loc.at[4]),
        pltpu.make_async_copy(integ.at[0], iv.at[pl.ds(0, slots)], loc.at[5]),
        pltpu.make_async_copy(integ.at[1], iv.at[pl.ds(slots, slots)], loc.at[6]),
    ]
    for c in local:
        c.start()
    iv[2 * slots] = jnp.zeros((tw, tw), BF16)
    acc[...] = jnp.zeros_like(acc)
    local[0].wait()
    local[1].wait()

    ha, hb = ra // 2, rb // 2

    def half_a(d):
        return pl.ds(d * ha, ha)

    def half_b(d):
        return pl.ds(d * hb, hb)

    def xfrom(d):
        return (xl, xr)[d]

    for d in range(2):
        ref = ga.at[z, xfrom(d)]
        rc(ref, ref, xa_s.at[d], xa_r.at[d], dev_x[d]).wait_recv()
        ref = ga.at[z, xfrom(d), half_a(d), :]
        rc(ref, ref, xa_s.at[2 + d], xa_r.at[2 + d], dev_x[d]).start()
    local[3].wait()
    local[4].wait()
    mrows = lm.shape[1]
    ntb = cv.shape[1]
    row = lax.broadcasted_iota(jnp.int32, (mrows, ntb), 0)
    col = lax.broadcasted_iota(jnp.int32, (mrows, ntb), 1)
    pick = (col == 2 * ((row // (2 * ps)) * NX + x) + (row // ps) % 2).astype(F32).astype(BF16)
    for side in range(2):
        lm[side] = jnp.dot(pick, cv[side], preferred_element_type=F32).astype(BF16)
    for d in range(2):
        ref = ga.at[z, xo, half_a(d), :]
        rc(ref, ref, xa_s.at[2 + d], xa_r.at[2 + d], dev_x[d]).wait_recv()

    def src_z(d, k):
        return (z + nz - k) % nz if d == 0 else (z + k) % nz

    def off(d, k):
        return (nz - k) % nz if d == 0 else k % nz

    def dirs(k):
        return (0,) if (isinstance(k, int) and k in (0, nh)) else (0, 1)

    kcols = nz * ps

    def mix_block(b):
        side, j = b // (2 * NX), b % 2
        xs = (b // 2) % NX
        vv = lax.broadcasted_iota(jnp.int32, (ntb, kcols), 0)
        cc = lax.broadcasted_iota(jnp.int32, (ntb, kcols), 1)
        spread = (vv == 2 * ((cc // ps) * NX + xs) + j).astype(F32).astype(BF16)
        full = jnp.dot(lm[side], spread, preferred_element_type=F32)
        rr = lax.broadcasted_iota(jnp.int32, (mrows, kcols), 0) % ps
        qq = lax.broadcasted_iota(jnp.int32, (mrows, kcols), 1) % ps
        km[b] = jnp.where(rr == qq, full, 0.0).astype(BF16)

    per_step = -(-4 * NX // nh)

    def ladder_terms(s):
        total = acc[...]
        for xs in range(NX):
            base = 2 * (s * NX + xs)
            w = jnp.concatenate(
                [
                    jnp.concatenate([iv[idx[i, base]], iv[idx[i, base + 1]]], axis=1)
                    for i in range(2)
                ],
                axis=0,
            )
            block = jnp.concatenate([ga[s, xs], gb[s, xs]], axis=0)
            total = total + nt_dot(block, w)
        acc[...] = total

    def step(k, first=False, last=False, tail=0):
        if tail == 0:
            for d in range(2):
                s = src_z(d, k)
                ref = gb.at[s, x]
                rc(ref, ref, zb_s.at[d, k], zb_r.at[d, k], dev_z[d]).wait_recv()
                if last:
                    ref = gb.at[s, x, half_b(d), :]
                rc(ref, ref, zb_s.at[d, k + 1], zb_r.at[d, k + 1], dev_z[d]).start()
            sends = (0, 1)
        elif tail == 1:
            s = src_z(0, nh)
            for d in range(2):
                ref = gb.at[s, x, half_b(d), :]
                rc(ref, ref, zb_s.at[d, nh], zb_r.at[d, nh], dev_z[d]).wait_recv()
            sends = (0,)
        else:
            sends = ()
        for side in sends:
            s, o = src_z(side, k), off(side, k)
            for d in range(2):
                ref = gb.at[s, x]
                rc(ref, ref, xb_s.at[o, d], xb_r.at[o, d], dev_x[d]).start()
        if first:
            for d in range(2):
                rc(ga.at[z], ga.at[z], za_s.at[d, 1], za_r.at[d, 1], dev_z[d]).start()
        elif tail <= 1:
            for d in range(2):
                ref = ga.at[src_z(d, k - 1)]
                rc(ref, ref, za_s.at[d, k - 1], za_r.at[d, k - 1], dev_z[d]).wait_recv()
                if tail == 1:
                    ref = ga.at[src_z(d, k - 1), pl.ds(2 * d, 2)]
                rc(ref, ref, za_s.at[d, k], za_r.at[d, k], dev_z[d]).start()
        elif tail == 2:
            for d in range(2):
                ref = ga.at[src_z(0, nh), pl.ds(2 * d, 2)]
                rc(ref, ref, za_s.at[d, nh], za_r.at[d, nh], dev_z[d]).wait_recv()
        if tail <= 2:
            for side in dirs(k - 1):
                s, o = src_z(side, k - 1), off(side, k - 1)
                for d in range(2):
                    ref = gb.at[s, xfrom(d)]
                    rc(ref, ref, xb_s.at[o, d], xb_r.at[o, d], dev_x[d]).wait_recv()
                    ref = gb.at[s, xfrom(d), half_b(d), :]
                    rc(ref, ref, xb_s.at[o, 2 + d], xb_r.at[o, 2 + d], dev_x[d]).start()
        if tail <= 1:
            @pl.loop(0, per_step)
            def _(i):
                b = (k - 1) * per_step + i
                mix_block(b)
        if first:
            for c in local[5:]:
                c.wait()
            return
        for side in dirs(k - 2):
            s, o = src_z(side, k - 2), off(side, k - 2)
            for d in range(2):
                ref = gb.at[s, xo, half_b(d), :]
                rc(ref, ref, xb_s.at[o, 2 + d], xb_r.at[o, 2 + d], dev_x[d]).wait_recv()
            ladder_terms(s)

    step(1, first=True, last=(nh == 2))
    if nh > 2:
        step(2, last=(nh == 3))
        if nh > 4:
            @pl.loop(3, nh - 1)
            def _(k):
                step(k)
        if nh > 3:
            step(nh - 1, last=True)
    for tail in (1, 2, 3):
        step(nh - 1 + tail, tail=tail)

    local[2].wait()
    ds[...] = (av[...].astype(F32) + acc[...]).astype(BF16)

    def order(i):
        return nh + (1 - 2 * (i % 2)) * ((i + 1) // 2)

    def rows_of(zz):
        return pl.ds(pl.multiple_of(zz * ps, ps), ps)

    def z_dev(o):
        return (z + o) % nz, {"tile": ((z + o) % nz) * NX + x}

    @pl.loop(0, nz - 1)
    def _(i):
        o = order(i)
        zz, dev = z_dev(o)
        rc(ds.at[rows_of(zz), :], e.at[0, x, z], zd_s.at[o], zd_r.at[o], dev).start()

    mine = pltpu.make_async_copy(ds.at[rows_of(z), :], e.at[0, x, z], loc.at[0])
    mine.start()
    mine.wait()

    def x_pass(o):
        zs = (z + nz - o) % nz
        for d in range(2):
            ref = e.at[0, x, zs]
            rc(ref, ref, xe_s.at[o, d], xe_r.at[o, d], dev_x[d]).start()

    def x_forward(o):
        zs = (z + nz - o) % nz
        for d in range(2):
            ref = e.at[0, xfrom(d), zs]
            rc(ref, ref, xe_s.at[o, d], xe_r.at[o, d], dev_x[d]).wait_recv()
        sgn = 1 - 2 * (o % 2)
        ref = e.at[0, (x + NX - sgn) % NX, zs]
        dev = {"tile": z * NX + (x + NX + sgn) % NX}
        rc(ref, ref, xe_s.at[o, 2], xe_r.at[o, 2], dev).start()

    x_pass(0)

    @pl.loop(0, nz - 1)
    def _(i):
        o = order(nz - 2 - i)
        zs = (z + nz - o) % nz
        ref = e.at[0, x, zs]
        rc(ref, ref, zd_s.at[o], zd_r.at[o], {"tile": zs * NX + x}).wait_recv()
        x_pass(o)

    def to_partner(dx):
        xs = (x + dx) % NX
        rc(e.at[0, xs], e.at[1, xs], pe_s.at[dx], pe_r.at[dx], dev_p).start()

    def mix(side, dx):
        xs = (x + dx) % NX
        for j in range(2):
            rhs = e[side, xs, :, :, j * tw : (j + 1) * tw].reshape(kcols, tw)
            b = (side * NX + xs) * 2 + j
            acc2[...] += jnp.dot(km[b], rhs, preferred_element_type=F32)

    to_partner(0)
    acc2[...] = jnp.zeros_like(acc2)
    mix(0, 0)
    x_forward(0)

    @pl.loop(0, nz - 1)
    def _(i):
        x_forward(order(nz - 2 - i))

    to_partner(1)
    to_partner(3)
    mix(0, 1)
    mix(0, 3)

    @pl.loop(0, nz)
    def _(o):
        zs = (z + nz - o) % nz
        ref = e.at[0, xo, zs]
        rc(ref, ref, xe_s.at[o, 2], xe_r.at[o, 2], dev_x[0]).wait_recv()

    to_partner(2)
    mix(0, 2)
    for dx in (0, 1, 3, 2):
        xs = (x + dx) % NX
        rc(e.at[0, xs], e.at[1, xs], pe_s.at[dx], pe_r.at[dx], dev_p).wait_recv()
        mix(1, dx)

    rs[...] = acc2[...].astype(BF16).reshape(rs.shape)

    @pl.loop(0, nz - 1)
    def _(i):
        o = order(i)
        zz, dev = z_dev(o)
        rc(rs.at[zz], r.at[z], zr_s.at[o], zr_r.at[o], dev).start()

    r[z] = rs[z]

    def sent(ref, sem):
        rc(ref, ref, sem, sem, dev_p).wait_send()

    for d in range(2):
        sent(own_a, xa_s.at[d])
        sent(ga.at[z, x, half_a(d), :], xa_s.at[2 + d])

        @pl.loop(1, nh)
        def _(k):
            sent(own_b, zb_s.at[d, k])
            sent(ga.at[z], za_s.at[d, k])

        sent(gb.at[z, x, half_b(d), :], zb_s.at[d, nh])
        sent(ga.at[z, pl.ds(0, 2)], za_s.at[d, nh])

    @pl.loop(0, nz)
    def _(o):
        for d in range(2):
            sent(gb.at[z, x], xb_s.at[o, d])
            sent(gb.at[z, x, half_b(d), :], xb_s.at[o, 2 + d])
            sent(e.at[0, x, z], xe_s.at[o, d])
        sent(e.at[0, x, z], xe_s.at[o, 2])

    for dx in range(NX):
        sent(e.at[0, 0], pe_s.at[dx])

    @pl.loop(1, nz)
    def _(o):
        zs = (z + nz - o) % nz
        rc(r.at[zs], r.at[zs], zr_s.at[o], zr_r.at[o], {"tile": zs * NX + x}).wait_recv()
        sent(e.at[0, x, z], zd_s.at[o])
        sent(rs.at[z], zr_s.at[o])

    for j in range(2):
        back = r[:, j].reshape(pairs, tw).astype(F32)
        lanes = slice(j * tw, (j + 1) * tw)
        out[:, lanes] = (acc[:, lanes] + back).astype(BF16)


def on_device(amplitudes, slot_cols, slot_count, integrals, cycle_same, cycle_cross):
    pairs, width = amplitudes.shape
    rows, slots, tw, _ = integrals.shape
    ntb = cycle_same.shape[1]
    nz = lax.axis_size("tile") // NX
    ps = pairs // nz
    ra = (3 * pairs // 8) // 32 * 32
    rb = pairs - ra
    nh = nz // 2
    live = lax.broadcasted_iota(jnp.int32, (rows, slots), 1) < slot_count[:, None]
    cols = jnp.where(live, slot_cols, ntb)
    hit = cols[:, :, None] == lax.broadcasted_iota(jnp.int32, (rows, slots, ntb), 2)
    number = lax.broadcasted_iota(jnp.int32, (rows, slots, ntb), 0) * slots
    number = number + lax.broadcasted_iota(jnp.int32, (rows, slots, ntb), 1)
    idx = jnp.min(jnp.where(hit, number, rows * slots), axis=1)

    dma = pltpu.SemaphoreType.DMA
    anyspace = pl.BlockSpec(memory_space=pl.ANY)
    vm = pltpu.VMEM
    mrows = nz * 2 * ps
    nb = 4 * NX
    per_step = -(-nb // nh)
    return pl.pallas_call(
        functools.partial(kernel, nz, ra),
        out_shape=jax.ShapeDtypeStruct((pairs, width), BF16),
        in_specs=[pl.BlockSpec(memory_space=pltpu.SMEM)] + [anyspace] * 4,
        out_specs=pl.BlockSpec(memory_space=pltpu.VMEM),
        scratch_shapes=[
            vm((nz, NX, ra, width), BF16),
            vm((nz, NX, rb, width), BF16),
            vm((rows * slots + 1, tw, tw), BF16),
            vm((2, ntb, ntb), BF16),
            vm((2, mrows, ntb), BF16),
            vm((per_step * nh, mrows, nz * ps), BF16),
            vm((pairs, width), BF16),
            vm((pairs, width), F32),
            vm((mrows, tw), F32),
            vm((pairs, width), BF16),
            vm((2, NX, nz, ps, width), BF16),
            vm((nz, 2, ps, tw), BF16),
            vm((nz, 2, ps, tw), BF16),
            dma((7,)),
            dma((2, nh + 1)), dma((2, nh + 1)),
            dma((2, nh + 1)), dma((2, nh + 1)),
            dma((4,)), dma((4,)),
            dma((nz, 4)), dma((nz, 4)),
            dma((nz,)), dma((nz,)),
            dma((nz, 3)), dma((nz, 3)),
            dma((NX,)), dma((NX,)),
            dma((nz,)), dma((nz,)),
        ],
        compiler_params=pltpu.CompilerParams(
            collective_id=0, has_side_effects=True, vmem_limit_bytes=48 << 20
        ),
    )(idx, amplitudes, integrals, cycle_same, cycle_cross)


def solution(mesh):
    in_specs = (
        P(None, ("sym", "tile")),
        P(("sym", "tile"), None),
        P(("sym", "tile")),
        P(("sym", "tile"), None, None, None),
        P("sym", None, None),
        P("sym", None, None),
    )
    return jax.shard_map(
        on_device, mesh=mesh, in_specs=in_specs, out_specs=P(None, ("sym", "tile")), check_vma=False
    )
```

time: 554 us -> 111 us (0.20)
  waiting for transfers between devices: 475 us -> 0 us
  Pallas kernels: 0 us -> 104 us
  local copies, waits for them, and re-layouts: 46.4 us -> 5.26 us
  matrix products: 15.3 us -> 0 us
  between operations: 13.2 us -> 0.02 us
    all_gather x3 -> x0, waiting for transfers between devices: 473 us -> none  [the longest x1 161 us: on_device(): gathered = lax.all_gather(amplitudes, 'tile', axis=1, tiled=True)]
    pallas_call x0 -> x1, Pallas kernels: none -> 104 us  [on_device(): pl.pallas_call(functools.partial(kernel, nz, ra), out_shape=jax.ShapeDtyp...]
    unnamed x13 -> x9, local copies, waits for them, and re-layouts: 21.5 us -> 5.26 us
    dot_general x4 -> x0, matrix products: 15.3 us -> none  [the longest x2 6.11 us: on_device(): jnp.einsum('psc,sac->pa', picked, integrals[tile_row], preferred_element_...]
    gather x2 -> x0, local copies, waits for them, and re-layouts: 12.8 us -> none  [on_device(): jnp.take(block_three, take_index[tile_row], axis=1, mode='fill', fill_val...]
    reshape x2 -> x0, local copies, waits for them, and re-layouts: 12.1 us -> none  [the longest x1 12 us: on_device(): block_three = gathered.reshape(pair_count, block_tiles, tile_width)]
  transfers between devices with their start and end apart: 4 -> 0, of which waited for: 4 -> 0; matrix products, arithmetic and copies ran while one was open for 3% -> 0% of each run, Pallas kernels for 0% -> 0%
where the time goes in v1:
time: 111 us; the launch traced here: 110 us
  Pallas kernels  104 us (94%)
  local copies, waits for them, and re-layouts  5.26 us (5%)
    pallas_call x1, Pallas kernels, on_device(): pl.pallas_call(functools.partial(kernel, nz, ra), out_shape=jax.ShapeDtyp...  104 us
    unnamed x9, local copies, waits for them, and re-layouts  5.26 us

profile of v1, /device:TPU:24, one launch (start us, length us, event | category | flops | bytes accessed | tf_op | source)
XLA Modules:
  0.0 110.3 jit_solution(15702789280792072780)
XLA Ops:
  0.0 0.8 compare_select_fusion
  0.8 0.1 select_reduce_fusion.idx
  0.9 0.0 copy-start
  0.9 2.2 %copy-done = bf16[2,64,128,128]{3,2,1,0:T(8,128)(2,1)S(1)} copy-done((bf16[2,64,128,128]{3,2,1,0:T(8,128)(2,1)S(1)}, bf16[2,64,128,128]{3,2,1,0:T(8,128)(2,1)}, u32[]{:S(2)}) %copy-start) | copy-done | bytes 4194328
  3.0 0.0 copy-start.1
  3.1 0.9 copy-done.1
  4.0 0.0 copy-start.2
  4.0 0.8 copy-done.2
  4.7 0.0 copy-start.3
  4.7 0.8 copy-done.3
  5.5 104.1 %shard_map.64 = bf16[256,256]{1,0:T(8,128)(2,1)S(1)} custom-call(s32[2,128]{1,0:T(2,128)S(1)} %select_reduce_fusion.idx, bf16[256,256]{1,0:T(8,128)(2,1)S(1)} %copy-done.1, bf16[2,64,128,128]{3,2,1,0:T(8,128)(2,1)S(1)} %copy-done, bf16[1,128,128]{2,1,0:T(8,128)(2,1)S(1)} %copy-done.2, bf16[1,128,128]{2,1,0:T(8,128)(2,1)S(1)} %copy-done.3), custom_call_target="tpu_custom_call" | custom-call | tf_op jit(solution)/shard_map/pallas_call | solution.py:373
  109.6 0.7 copy.8
  (1 shorter events, 0.0 us)
Async XLA Ops:
  0.9 2.2 %copy-start = (bf16[2,64,128,128]{3,2,1,0:T(8,128)(2,1)S(1)}, bf16[2,64,128,128]{3,2,1,0:T(8,128)(2,1)}, u32[]{:S(2)}) copy-start(bf16[2,64,128,128]{3,2,1,0:T(8,128)(2,1)} %integ.1) | copy-start | bytes 12582916
  3.0 0.9 copy-start.1
  4.0 0.8 copy-start.2
  4.7 0.8 copy-start.3

commit v2 on v1

--- a/solution.py
+++ b/solution.py
@@ -8,6 +8,8 @@
 from jax.sharding import PartitionSpec as P
 
 MESH = pl.DeviceIdType.MESH
+A_LAG = 1
+X_LAG = 1
 NX = 4
 F32 = jnp.float32
 BF16 = jnp.bfloat16
@@ -55,6 +57,7 @@
         rc(own_b, gb.at[z, x], zb_s.at[d, 1], zb_r.at[d, 1], dev_z[d]).start()
         rc(own_a, ga.at[z, x], xa_s.at[d], xa_r.at[d], dev_x[d]).start()
     for d in range(2):
+        rc(own_a, ga.at[z, x], za_s.at[d, 1, 0], za_r.at[d, 1, 0], dev_z[d]).start()
         rc(own_b, gb.at[z, x], xb_s.at[0, d], xb_r.at[0, d], dev_x[d]).start()
     local = [
         pltpu.make_async_copy(own_a, ga.at[z, x], loc.at[0]),
@@ -69,8 +72,6 @@
         c.start()
     iv[2 * slots] = jnp.zeros((tw, tw), BF16)
     acc[...] = jnp.zeros_like(acc)
-    local[0].wait()
-    local[1].wait()
 
     ha, hb = ra // 2, rb // 2
 
@@ -82,10 +83,19 @@
 
     def xfrom(d):
         return (xl, xr)[d]
+
+    parts = (x, xl, xr, xo)
+    final = ((0, 3), (1, 2))
+
+    def send_a(d, s, j, k):
+        ref = ga.at[s, parts[j]]
+        rc(ref, ref, za_s.at[d, k, j], za_r.at[d, k, j], dev_z[d]).start()
 
     for d in range(2):
         ref = ga.at[z, xfrom(d)]
         rc(ref, ref, xa_s.at[d], xa_r.at[d], dev_x[d]).wait_recv()
+        for dz in range(2):
+            send_a(dz, z, 1 + d, 1)
         ref = ga.at[z, xfrom(d), half_a(d), :]
         rc(ref, ref, xa_s.at[2 + d], xa_r.at[2 + d], dev_x[d]).start()
     local[3].wait()
@@ -97,9 +107,8 @@
     pick = (col == 2 * ((row // (2 * ps)) * NX + x) + (row // ps) % 2).astype(F32).astype(BF16)
     for side in range(2):
         lm[side] = jnp.dot(pick, cv[side], preferred_element_type=F32).astype(BF16)
-    for d in range(2):
-        ref = ga.at[z, xo, half_a(d), :]
-        rc(ref, ref, xa_s.at[2 + d], xa_r.at[2 + d], dev_x[d]).wait_recv()
+    local[0].wait()
+    local[1].wait()
 
     def src_z(d, k):
         return (z + nz - k) % nz if d == 0 else (z + k) % nz
@@ -140,78 +149,91 @@
             total = total + nt_dot(block, w)
         acc[...] = total
 
-    def step(k, first=False, last=False, tail=0):
-        if tail == 0:
+    def hop_a(k, j, last, ended):
+        for d in range(2):
+            s = src_z(d, k)
+            if ended and j not in final[d]:
+                continue
+            ref = ga.at[s, parts[j]]
+            rc(ref, ref, za_s.at[d, k, j], za_r.at[d, k, j], dev_z[d]).wait_recv()
+            if not ended and (not last or j in final[d]):
+                send_a(d, s, j, k + 1)
+
+    def step(k):
+        inner = not isinstance(k, int)
+
+        def within(v, low, high):
+            return inner or low <= v <= high
+
+        if within(k, 1, nh - 1):
             for d in range(2):
                 s = src_z(d, k)
                 ref = gb.at[s, x]
                 rc(ref, ref, zb_s.at[d, k], zb_r.at[d, k], dev_z[d]).wait_recv()
-                if last:
+                if not inner and k == nh - 1:
                     ref = gb.at[s, x, half_b(d), :]
                 rc(ref, ref, zb_s.at[d, k + 1], zb_r.at[d, k + 1], dev_z[d]).start()
-            sends = (0, 1)
-        elif tail == 1:
+        elif k == nh:
             s = src_z(0, nh)
             for d in range(2):
                 ref = gb.at[s, x, half_b(d), :]
                 rc(ref, ref, zb_s.at[d, nh], zb_r.at[d, nh], dev_z[d]).wait_recv()
-            sends = (0,)
-        else:
-            sends = ()
-        for side in sends:
-            s, o = src_z(side, k), off(side, k)
-            for d in range(2):
-                ref = gb.at[s, x]
-                rc(ref, ref, xb_s.at[o, d], xb_r.at[o, d], dev_x[d]).start()
-        if first:
-            for d in range(2):
-                rc(ga.at[z], ga.at[z], za_s.at[d, 1], za_r.at[d, 1], dev_z[d]).start()
-        elif tail <= 1:
-            for d in range(2):
-                ref = ga.at[src_z(d, k - 1)]
-                rc(ref, ref, za_s.at[d, k - 1], za_r.at[d, k - 1], dev_z[d]).wait_recv()
-                if tail == 1:
-                    ref = ga.at[src_z(d, k - 1), pl.ds(2 * d, 2)]
-                rc(ref, ref, za_s.at[d, k], za_r.at[d, k], dev_z[d]).start()
-        elif tail == 2:
-            for d in range(2):
-                ref = ga.at[src_z(0, nh), pl.ds(2 * d, 2)]
-                rc(ref, ref, za_s.at[d, nh], za_r.at[d, nh], dev_z[d]).wait_recv()
-        if tail <= 2:
-            for side in dirs(k - 1):
-                s, o = src_z(side, k - 1), off(side, k - 1)
+        if within(k, 1, nh):
+            for side in dirs(k):
+                s, o = src_z(side, k), off(side, k)
+                for d in range(2):
+                    ref = gb.at[s, x]
+                    rc(ref, ref, xb_s.at[o, d], xb_r.at[o, d], dev_x[d]).start()
+        kx = k - X_LAG
+        if within(kx, 0, nh):
+            for side in dirs(kx):
+                s, o = src_z(side, kx), off(side, kx)
                 for d in range(2):
                     ref = gb.at[s, xfrom(d)]
                     rc(ref, ref, xb_s.at[o, d], xb_r.at[o, d], dev_x[d]).wait_recv()
                     ref = gb.at[s, xfrom(d), half_b(d), :]
                     rc(ref, ref, xb_s.at[o, 2 + d], xb_r.at[o, 2 + d], dev_x[d]).start()
-        if tail <= 1:
+        ka = k - A_LAG
+        if within(ka, 1, nh):
+            for j in range(3):
+                hop_a(ka, j, not inner and ka == nh - 1, not inner and ka == nh)
+        ko = k - 1
+        if not inner and ko == 0:
+            for d in range(2):
+                ref = ga.at[z, xo, half_a(d), :]
+                rc(ref, ref, xa_s.at[2 + d], xa_r.at[2 + d], dev_x[d]).wait_recv()
+            for d in range(2):
+                send_a(d, z, 3, 1)
+        elif within(ko, 1, nh):
+            hop_a(ko, 3, not inner and ko == nh - 1, not inner and ko == nh)
+        if within(k, 1, nh):
             @pl.loop(0, per_step)
             def _(i):
                 b = (k - 1) * per_step + i
                 mix_block(b)
-        if first:
+        kl = k - X_LAG - 1
+        if not inner and kl == 0:
             for c in local[5:]:
                 c.wait()
-            return
-        for side in dirs(k - 2):
-            s, o = src_z(side, k - 2), off(side, k - 2)
-            for d in range(2):
-                ref = gb.at[s, xo, half_b(d), :]
-                rc(ref, ref, xb_s.at[o, 2 + d], xb_r.at[o, 2 + d], dev_x[d]).wait_recv()
-            ladder_terms(s)
-
-    step(1, first=True, last=(nh == 2))
-    if nh > 2:
-        step(2, last=(nh == 3))
-        if nh > 4:
-            @pl.loop(3, nh - 1)
-            def _(k):
-                step(k)
-        if nh > 3:
-            step(nh - 1, last=True)
-    for tail in (1, 2, 3):
-        step(nh - 1 + tail, tail=tail)
+        if within(kl, 0, nh):
+            for side in dirs(kl):
+                s, o = src_z(side, kl), off(side, kl)
+                for d in range(2):
+                    ref = gb.at[s, xo, half_b(d), :]
+                    rc(ref, ref, xb_s.at[o, 2 + d], xb_r.at[o, 2 + d], dev_x[d]).wait_recv()
+                ladder_terms(s)
+
+    ends = nh + X_LAG + 2
+    begin = min(X_LAG + 2, ends)
+    stop = max(begin, nh - 1)
+    for k in range(1, begin):
+        step(k)
+    if stop > begin:
+        @pl.loop(begin, stop)
+        def _(k):
+            step(k)
+    for k in range(stop, ends):
+        step(k)
 
     local[2].wait()
     ds[...] = (av[...].astype(F32) + acc[...]).astype(BF16)
@@ -319,10 +341,12 @@
         @pl.loop(1, nh)
         def _(k):
             sent(own_b, zb_s.at[d, k])
-            sent(ga.at[z], za_s.at[d, k])
+            for j in range(NX):
+                sent(own_a, za_s.at[d, k, j])
 
         sent(gb.at[z, x, half_b(d), :], zb_s.at[d, nh])
-        sent(ga.at[z, pl.ds(0, 2)], za_s.at[d, nh])
+        for j in final[d]:
+            sent(own_a, za_s.at[d, nh, j])
 
     @pl.loop(0, nz)
     def _(o):
@@ -391,7 +415,7 @@
             vm((nz, 2, ps, tw), BF16),
             dma((7,)),
             dma((2, nh + 1)), dma((2, nh + 1)),
-            dma((2, nh + 1)), dma((2, nh + 1)),
+            dma((2, nh + 1, NX)), dma((2, nh + 1, NX)),
             dma((4,)), dma((4,)),
             dma((nz, 4)), dma((nz, 4)),
             dma((nz,)), dma((nz,)),
@@ -400,7 +424,7 @@
             dma((nz,)), dma((nz,)),
         ],
         compiler_params=pltpu.CompilerParams(
-            collective_id=0, has_side_effects=True, vmem_limit_bytes=48 << 20
+            collective_id=0, has_side_effects=True, vmem_limit_bytes=67043328
         ),
     )(idx, amplitudes, integrals, cycle_same, cycle_cross)
 

time: 111 us -> 97.2 us (0.88)
  Pallas kernels: 104 us -> 94 us
  local copies, waits for them, and re-layouts: 5.26 us -> 1.57 us
    pallas_call x1, Pallas kernels: 104 us -> 94 us  [on_device(): pl.pallas_call(functools.partial(kernel, nz, ra), out_shape=jax.ShapeDtyp...]
    unnamed x9 -> x1, local copies, waits for them, and re-layouts: 5.26 us -> 1.57 us
where the time goes in v2:
time: 97.2 us; the launch traced here: 97 us
  Pallas kernels  94 us (97%)
  local copies, waits for them, and re-layouts  1.57 us (2%)
  other arithmetic  1.42 us (1%)
    pallas_call x1, Pallas kernels, on_device(): pl.pallas_call(functools.partial(kernel, nz, ra), out_shape=jax.ShapeDtyp...  94 us

profile of v2, /device:TPU:24, one launch (start us, length us, event | category | flops | bytes accessed | tf_op | source)
XLA Modules:
  0.0 97.0 jit_solution(10792146773394349579)
XLA Ops:
  0.0 0.8 compare_select_fusion
  0.8 0.7 select_reduce_fusion.idx
  1.4 94.0 %shard_map.64 = bf16[256,256]{1,0:T(8,128)(2,1)} custom-call(s32[2,128]{1,0:T(2,128)} %select_reduce_fusion.idx, bf16[256,256]{1,0:T(8,128)(2,1)} %amps.1, bf16[2,64,128,128]{3,2,1,0:T(8,128)(2,1)} %integ.1, bf16[1,128,128]{2,1,0:T(8,128)(2,1)} %same.1, bf16[1,128,128]{2,1,0:T(8,128)(2,1)} %cross.1), custom_call_target="tpu_custom_call" | custom-call | tf_op jit(solution)/shard_map/pallas_call | solution.py:397
  95.5 1.6 %copy.8 = bf16[256,256]{1,0:T(8,128)(2,1)} copy(bf16[256,256]{1,0:T(8,128)(2,1)} %shard_map.64) | data formatting | bytes 262144
  (1 shorter events, 0.0 us)

commit v3 on v2

--- a/solution.py
+++ b/solution.py
@@ -295,8 +295,6 @@
             acc2[...] += jnp.dot(km[b], rhs, preferred_element_type=F32)
 
     to_partner(0)
-    acc2[...] = jnp.zeros_like(acc2)
-    mix(0, 0)
     x_forward(0)
 
     @pl.loop(0, nz - 1)
@@ -305,6 +303,8 @@
 
     to_partner(1)
     to_partner(3)
+    acc2[...] = jnp.zeros_like(acc2)
+    mix(0, 0)
     mix(0, 1)
     mix(0, 3)
 

time: 97.2 us -> 97.2 us (level)
  no operation moved by 1% of the time
where the time goes in v3:
time: 97.2 us; the launch traced here: 97 us
  Pallas kernels  94 us (97%)
  local copies, waits for them, and re-layouts  1.57 us (2%)
  other arithmetic  1.42 us (1%)
    pallas_call x1, Pallas kernels, on_device(): pl.pallas_call(functools.partial(kernel, nz, ra), out_shape=jax.ShapeDtyp...  94 us

profile of v3, /device:TPU:24, one launch (start us, length us, event | category | flops | bytes accessed | tf_op | source)
XLA Modules:
  0.0 97.0 jit_solution(1651154695829673237)
XLA Ops:
  0.0 0.8 compare_select_fusion
  0.8 0.7 select_reduce_fusion.idx
  1.4 94.0 %shard_map.64 = bf16[256,256]{1,0:T(8,128)(2,1)} custom-call(s32[2,128]{1,0:T(2,128)} %select_reduce_fusion.idx, bf16[256,256]{1,0:T(8,128)(2,1)} %amps.1, bf16[2,64,128,128]{3,2,1,0:T(8,128)(2,1)} %integ.1, bf16[1,128,128]{2,1,0:T(8,128)(2,1)} %same.1, bf16[1,128,128]{2,1,0:T(8,128)(2,1)} %cross.1), custom_call_target="tpu_custom_call" | custom-call | tf_op jit(solution)/shard_map/pallas_call | solution.py:397
  95.5 1.6 %copy.8 = bf16[256,256]{1,0:T(8,128)(2,1)} copy(bf16[256,256]{1,0:T(8,128)(2,1)} %shard_map.64) | data formatting | bytes 262144
  (1 shorter events, 0.0 us)
